TPU v7x, 32 devices: a whole 2x2x4 slice. The times are simulated.
32 devices in a mesh: parts: 2 (over y), rng: 8 (over z, x), chan: 2 (over core).
Axes of the slice: x: 2, y: 2, z: 4, core: 2. Of those that a mesh axis runs over, the one named last changes fastest.
Arguments:
- snapshots: bfloat16 [8, 2, 16384, 192], P('parts', None, 'rng', 'chan'), parts along dimension 0, may hold values from -24 to 24
- train_gates: int32 [8, 128], P('parts', 'rng'), parts along dimension 0, may hold values from 0 to 2047
- guard_keep: int32 [8, 128], P('parts', 'rng'), parts along dimension 0, may hold values 0 or 1
- beam_cells: int32 [8, 16], P('parts'), parts along dimension 0, may hold values from 0 to 767
Outputs:
- beam_out: bfloat16 [8, 2, 16, 16384], P('parts', None, None, ('rng', 'chan')), parts along dimension 0
- weights: float32 [8, 16, 384], P('parts'), parts along dimension 0
There are 2 independent parts, one for each index of `parts`. A program takes and returns all parts, laid end to end along the dimension named above; each array names one. Nothing has to cross between parts.
Inputs may be any that keep to these rules, and one draw needn't show every extreme that they name: `train_gates`: an offset into the 2048 gates of the range group that holds the entry. `beam_cells`: angle cell times 12 plus Doppler cell.
All inputs are finite; a program needn't handle non-finite values. No bound on the sum of `guard_keep` on one device may be relied on, other than what follows from the above.
Results may differ from a plain program's by a relative error of at most 0.01225.
Values may be sent and summed in bfloat16 or wider, within the bound.
A program may use at most 64 MiB of HBM per device.

v0:
```python
import math
import jax
import jax.numpy as jnp
from jax import lax
from jax.sharding import PartitionSpec as P

ELEM = 16
PULSE = 12
CH = 192
ANGLES = 64
LOADING = 0.05


def steering(cells):
    angle_cell = (cells // PULSE).astype(jnp.float32)
    doppler_cell = (cells % PULSE).astype(jnp.float32)
    sine_angle = -1.0 + (2.0 * angle_cell + 1.0) / ANGLES
    doppler_freq = (doppler_cell + 0.5) / PULSE - 0.5
    channel = jnp.arange(CH, dtype=jnp.int32)
    element = (channel % ELEM).astype(jnp.float32)
    pulse_index = (channel // ELEM).astype(jnp.float32)
    phases = (
        math.pi * element[None, :] * sine_angle[:, None]
        + 2.0 * math.pi * pulse_index[None, :] * doppler_freq[:, None]
    )
    norm_scale = 1.0 / math.sqrt(CH)
    return jnp.concatenate([jnp.cos(phases), jnp.sin(phases)], axis=1) * norm_scale


def gram_product(left, right):
    return lax.dot_general(
        left, right, (((0,), (0,)), ((), ())), preferred_element_type=jnp.float32
    )


def apply_taps(beam_taps, samples):
    return lax.dot_general(
        beam_taps, samples, (((0,), (1,)), ((), ())), preferred_element_type=jnp.float32
    )


def solve_weights(covariance, steer_vec):
    matrix_order = covariance.shape[0]
    loading = LOADING * jnp.trace(covariance) / matrix_order + 1e-06
    loaded = covariance + loading * jnp.eye(matrix_order, dtype=jnp.float32)
    factor = jnp.linalg.cholesky(loaded)
    forward = lax.linalg.triangular_solve(factor, steer_vec.T, left_side=True, lower=True)
    solved = lax.linalg.triangular_solve(
        factor, forward, left_side=True, lower=True, transpose_a=True
    )
    unit_gain = jnp.sum(steer_vec.T * solved, axis=0)
    return (solved / unit_gain[None, :]).T


def make_taps(weight_rows):
    weights = weight_rows.T
    half_order = weights.shape[0] // 2
    rotated = jnp.concatenate([-weights[half_order:], weights[:half_order]], axis=0)
    return jnp.concatenate([weights, rotated], axis=1).astype(jnp.bfloat16)


def per_device(snapshots, train_gates, guard_keep, beam_cells):
    groups = snapshots.shape[0]
    shard_width = snapshots.shape[3]
    chan_count = lax.axis_size("chan")
    chan_place = lax.axis_index("chan")
    full_width = shard_width * chan_count
    beam_count = beam_cells.shape[1]
    picked = jax.vmap(lambda cube, chosen: jnp.take(cube, chosen, axis=1))(snapshots, train_gates)
    picked = picked * guard_keep[:, None, :, None].astype(jnp.bfloat16)
    training = lax.all_gather(picked, "chan", axis=3, tiled=True)
    training = lax.all_gather(training, "rng", axis=2, tiled=True)
    cov_list = []
    for bin_group in range(groups):
        chosen = training[bin_group]
        direct = jnp.concatenate([chosen[0], chosen[1]], axis=1)
        turned = jnp.concatenate([-chosen[1], chosen[0]], axis=1)
        covariance = gram_product(direct, direct) + gram_product(turned, turned)
        cov_list.append(covariance)
    cov_stack = jnp.stack(cov_list)
    steer_stack = jax.vmap(steering)(beam_cells)
    rng_place = lax.axis_index("rng")
    group_pick = rng_place % groups
    own_cov = lax.dynamic_index_in_dim(cov_stack, group_pick, 0, keepdims=False)
    own_steer = lax.dynamic_index_in_dim(steer_stack, group_pick, 0, keepdims=False)
    own_weights = solve_weights(own_cov, own_steer)
    group_ids = jnp.arange(groups, dtype=jnp.int32)
    owner = jnp.where((group_ids == group_pick) & (rng_place < groups), 1.0, 0.0).astype(
        jnp.float32
    )
    weight_stack = lax.psum(owner[:, None, None] * own_weights[None], "rng")
    taps_stack = jax.vmap(make_taps)(weight_stack)
    beam_list = []
    for bin_group in range(groups):
        beam_taps = taps_stack[bin_group]
        real_taps = lax.dynamic_slice_in_dim(beam_taps, chan_place * shard_width, shard_width, 0)
        imag_taps = lax.dynamic_slice_in_dim(
            beam_taps, full_width + chan_place * shard_width, shard_width, 0
        )
        partial_out = apply_taps(real_taps, snapshots[bin_group, 0]) + apply_taps(
            imag_taps, snapshots[bin_group, 1]
        )
        outputs = lax.psum_scatter(partial_out, "chan", scatter_dimension=1, tiled=True)
        beam_list.append(outputs.reshape(2, beam_count, outputs.shape[1]).astype(jnp.bfloat16))
    return (jnp.stack(beam_list), weight_stack)


def solution(mesh):
    placed = (
        P("parts", None, "rng", "chan"),
        P("parts", "rng"),
        P("parts", "rng"),
        P("parts", None),
    )
    return jax.shard_map(
        per_device,
        mesh=mesh,
        in_specs=placed,
        out_specs=(P("parts", None, None, ("rng", "chan")), P("parts", None, None)),
        check_vma=False,
    )
```

profile of v0, /device:TPU:0, one launch (start us, length us, event | category | flops | bytes accessed | tf_op | source)
XLA Modules:
  0.0 298.7 jit_solution(11843807177407830651)
XLA Ops:
  7.2 0.7 bitcast_or_fusion
  7.9 0.7 compare_and_fusion
  8.6 11.0 %copy.52 = bf16[4,2,2048,96]{3,1,2,0:T(2,128)(2,1)} copy(bf16[4,2,2048,96]{2,3,1,0:T(8,128)(2,1)} %param.4) | data formatting | bytes 6291456 | tf_op args[0]
  19.7 2.9 gather_fusion
  22.9 2.2 all_gather.6
  25.4 33.1 %all_gather.7 = bf16[4,2,128,192]{3,0,1,2:T(4,128)(2,1)S(1)} all-gather(bf16[4,2,16,192]{3,0,1,2:T(4,128)(2,1)S(1)} %copy.55), channel_id=1, replica_groups=mesh['parts'=2,'rng'=8,'chan'=2] {'rng'}, dimensions={2}, use_global_device_ids=true | all-gather | bytes 442368 | tf_op jit(solution)/shard_map/all_gather | solution.py:72
  58.5 0.8 fusion.132
  63.0 0.7 fusion.8
  64.7 11.7 %cholesky.76 = f32[128,128]{1,0:T(8,128)S(1)} custom-call(f32[128,128]{1,0:T(8,128)S(1)} %cholesky.189), custom_call_target="Cholesky" | custom-call | tf_op jit(solution)/shard_map/jit(cholesky)/cholesky | solution.py:46
  76.5 9.8 %custom-call.24 = f32[1,128,128]{1,2,0:T(8,128)S(1)} custom-call(f32[1,128,128]{2,1,0:T(8,128)S(1)} %get-tuple-element.51), custom_call_target="InvertDiagBlocksLowerTriangular" | custom-call | tf_op jit(solution)/shard_map/jit(cholesky)/cholesky | solution.py:46
  86.9 11.9 %cholesky.160 = f32[128,128]{1,0:T(8,128)S(1)} custom-call(f32[128,128]{1,0:T(8,128)S(1)} %cholesky.193), custom_call_target="Cholesky" | custom-call | tf_op jit(solution)/shard_map/jit(cholesky)/cholesky | solution.py:46
  99.1 9.8 %custom-call.25 = f32[1,128,128]{1,2,0:T(8,128)S(1)} custom-call(f32[1,128,128]{2,1,0:T(8,128)S(1)} %get-tuple-element.49), custom_call_target="InvertDiagBlocksLowerTriangular" | custom-call | tf_op jit(solution)/shard_map/jit(cholesky)/cholesky | solution.py:46
  109.3 0.8 copy-done.1
  110.1 1.4 convolution_subtract_fusion.1
  111.5 11.7 %cholesky.179 = f32[128,128]{1,0:T(8,128)S(1)} custom-call(f32[128,128]{1,0:T(8,128)S(1)} %convolution_subtract_fusion.1), custom_call_target="Cholesky" | custom-call | tf_op jit(solution)/shard_map/jit(cholesky)/cholesky | solution.py:46
  123.4 0.6 compare_reduce_fusion
  124.0 0.6 constant_dynamic-update-slice_fusion.1
  124.6 0.7 compare_reduce_fusion.1
  127.2 1.9 select_select_fusion
  129.1 9.3 %while.1 = (s32[]{:T(128)}, f32[384,384]{0,1:T(8,128)}, s32[3,2]{0,1:T(2,128)S(1)}, f32[3,128,128]{2,1,0:T(8,128)S(1)}, s32[]{:T(128)}) while((s32[]{:T(128)}, f32[384,384]{0,1:T(8,128)}, s32[3,2]{0,1:T(2,128)S(1)}, f32[3,128,128]{2,1,0:T(8,128)S(1)}, s32[]{:T(128)}) %tuple.43), condition=%wide.while_cond, body=%wide.while_body.sunk | while | flops 2 | bytes 393321 | solution.py:48
  129.8 2.3 dynamic-slice.15
  132.3 0.6 fusion.143
  132.9 2.3 dynamic-slice.15
  135.5 0.6 fusion.143
  136.1 2.3 dynamic-slice.15
  138.5 29.5 %custom-call.26 = f32[3,128,128]{1,2,0:T(8,128)S(1)} custom-call(f32[3,128,128]{2,1,0:T(8,128)S(1)} %get-tuple-element.9), custom_call_target="InvertDiagBlocksLowerTriangular" | custom-call | tf_op jit(solution)/shard_map/triangular_solve | solution.py:48
  168.6 1.0 convolution_subtract_fusion.5
  169.8 1.1 convolution_subtract_fusion.4
  171.3 1.0 convolution_subtract_fusion.3
  172.5 1.1 convolution_subtract_fusion.2
  174.1 0.7 broadcast_multiply_fusion
  174.9 71.2 %all-reduce.3.cloned.1.call-done = f32[4,16,384]{2,1,0:T(8,128)} async-done(((f32[4,16,384]{2,1,0:T(8,128)}), f32[4,16,384]{2,1,0:T(8,128)}) %all-reduce.3.cloned.1.call-update) | async-done | bytes 98320 | tf_op jit(solution)/shard_map/psum | solution.py:91
  246.1 0.9 bitcast_convert_fusion
  247.1 0.9 fusion.62
  248.3 1.0 convolution_add_fusion.3
  249.7 1.0 convolution_add_fusion.2
  250.9 1.0 convolution_add_fusion.1
  252.2 1.0 convolution_add_fusion
  253.2 3.1 %reduce-scatter.5.cloned.1.call-done = f32[32,1024]{1,0:T(8,128)} async-done(((f32[32,2048]{1,0:T(8,128)}), f32[32,1024]{1,0:T(8,128)}) %reduce-scatter.5.cloned.1.call-update) | async-done | bytes 131088 | tf_op jit(solution)/shard_map/reduce_scatter | solution.py:103
  256.3 0.9 convert_element_type.85
  257.2 10.2 %reduce-scatter.7.cloned.1.call-done = f32[32,1024]{1,0:T(8,128)} async-done(((f32[32,2048]{1,0:T(8,128)}), f32[32,1024]{1,0:T(8,128)}) %reduce-scatter.7.cloned.1.call-update) | async-done | bytes 131088 | tf_op jit(solution)/shard_map/reduce_scatter | solution.py:103
  267.4 0.9 convert_element_type.87
  268.3 10.1 %reduce-scatter.9.cloned.1.call-done = f32[32,1024]{1,0:T(8,128)} async-done(((f32[32,2048]{1,0:T(8,128)}), f32[32,1024]{1,0:T(8,128)}) %reduce-scatter.9.cloned.1.call-update) | async-done | bytes 131088 | tf_op jit(solution)/shard_map/reduce_scatter | solution.py:103
  278.4 0.9 convert_element_type.89
  279.3 10.6 %reduce-scatter.11.cloned.1.call-done = f32[32,1024]{1,0:T(8,128)} async-done(((f32[32,2048]{1,0:T(8,128)}), f32[32,1024]{1,0:T(8,128)}) %reduce-scatter.11.cloned.1.call-update) | async-done | bytes 131088 | tf_op jit(solution)/shard_map/reduce_scatter | solution.py:103
  289.9 0.9 convert_element_type.91
  290.8 0.7 pad_maximum_fusion
  291.6 0.6 copy.96
  (100 shorter events, 10.4 us)
Async XLA Ops:
  7.2 239.0 %all-reduce.3.cloned.1.call-start = ((), (), s32[]{:S(2)}) async-start(), calls=%async_computation.4 | async-start | bytes 196608 | tf_op jit(solution)/shard_map/psum | solution.py:91
  8.6 14.0 %copy-start.5 = (s32[4,16]{1,0:T(4,128)S(1)}, s32[4,16]{1,0:T(4,128)}, u32[]{:S(2)}) copy-start(s32[4,16]{1,0:T(4,128)} %param.6) | copy-start | bytes 772
  64.7 44.3 %copy-start.2 = (f32[384,384]{1,0:T(8,128)}, f32[384,384]{1,0:T(8,128)S(1)}, u32[]{:S(2)}) copy-start(f32[384,384]{1,0:T(8,128)S(1)} %fusion.7) | copy-start | bytes 1769476
  86.6 81.4 %copy-start.4 = (s32[4,16]{1,0:T(4,128)S(1)}, s32[4,16]{1,0:T(4,128)}, u32[]{:S(2)}) copy-start(s32[4,16]{1,0:T(4,128)} %param.7) | copy-start | bytes 772
  109.3 0.8 copy-start.1
  110.1 138.0 %copy-start = (bf16[4,2,2048,96]{2,3,1,0:T(8,128)(2,1)S(1)}, bf16[4,2,2048,96]{2,3,1,0:T(8,128)(2,1)}, u32[]{:S(2)}) copy-start(bf16[4,2,2048,96]{2,3,1,0:T(8,128)(2,1)} %param.4) | copy-start | bytes 9437188
  174.9 81.4 %reduce-scatter.5.cloned.1.call-start = ((), (), s32[]{:S(2)}) async-start(), calls=%async_computation.5 | async-start | bytes 393216 | tf_op jit(solution)/shard_map/reduce_scatter | solution.py:103
  249.3 18.1 %reduce-scatter.7.cloned.1.call-start = ((), (), s32[]{:S(2)}) async-start(), calls=%async_computation.6 | async-start | bytes 393216 | tf_op jit(solution)/shard_map/reduce_scatter | solution.py:103
  249.6 41.9 %copy-start.3 = (f32[4,16,384]{2,1,0:T(8,128)S(1)}, f32[4,16,384]{2,1,0:T(8,128)}, u32[]{:S(2)}) copy-start(f32[4,16,384]{2,1,0:T(8,128)} %all-reduce.3.cloned.1.call-done) | copy-start | bytes 294916
  250.6 27.7 %reduce-scatter.9.cloned.1.call-start = ((), (), s32[]{:S(2)}) async-start(), calls=%async_computation.7 | async-start | bytes 393216 | tf_op jit(solution)/shard_map/reduce_scatter | solution.py:103
  251.9 38.0 %reduce-scatter.11.cloned.1.call-start = ((), (), s32[]{:S(2)}) async-start(), calls=%async_computation.8 | async-start | bytes 393216 | tf_op jit(solution)/shard_map/reduce_scatter | solution.py:103
Sparse Core Ops, SparseCore 0:
  175.0 71.1 all-reduce.2
  249.5 6.7 reduce-scatter.4
  258.5 8.8 reduce-scatter.6
  269.5 8.8 reduce-scatter.8
  281.0 8.8 reduce-scatter.10
where the time goes:
time: 300 us; the launch traced here: 299 us
  waiting for transfers between devices  105 us (35%)
  other arithmetic  97.9 us (33%)
  blocking collectives  35.3 us (12%)
  local copies, waits for them, and re-layouts  28.6 us (10%)
  between operations  16.8 us (6%)
  matrix products  14.6 us (5%)
    psum x1, waiting for transfers between devices, per_device(): weight_stack = lax.psum(owner[:, None, None] * own_weights[None], 'rng')  71.2 us
    another operation x10, other arithmetic, solve_weights(): factor = jnp.linalg.cholesky(loaded)  56.3 us
    reduce_scatter x4, waiting for transfers between devices, per_device(): lax.psum_scatter(partial_out, 'chan', scatter_dimension=1, tiled=True)  33.9 us
    all_gather x1, blocking collectives, per_device(): training = lax.all_gather(training, 'rng', axis=2, tiled=True)  33.1 us
    another operation x3, other arithmetic, solve_weights(): lax.linalg.triangular_solve(factor, forward, left_side=True, lower=True,...  31.4 us
    unnamed x22, local copies, waits for them, and re-layouts  13.5 us
    another operation x15, local copies, waits for them, and re-layouts  9.25 us
  transfers between devices with their start and end apart: 5, of which 5 were waited for; matrix products, arithmetic and copies ran while one was open for 2% of the time, Pallas kernels for 0%

commit v1 on v0

--- a/solution.py
+++ b/solution.py
@@ -3,6 +3,7 @@
 import jax.numpy as jnp
 from jax import lax
 from jax.sharding import PartitionSpec as P
+from jax.lax import all_gather
 
 ELEM = 16
 PULSE = 12
@@ -88,7 +89,9 @@
     owner = jnp.where((group_ids == group_pick) & (rng_place < groups), 1.0, 0.0).astype(
         jnp.float32
     )
-    weight_stack = lax.psum(owner[:, None, None] * own_weights[None], "rng")
+    block_here = owner[:, None, None] * own_weights[None]
+    piece_now = all_gather(block_here, "rng")
+    weight_stack = jnp.sum(piece_now, 0)
     taps_stack = jax.vmap(make_taps)(weight_stack)
     beam_list = []
     for bin_group in range(groups):

time: 300 us -> 261 us (0.87)
  waiting for transfers between devices: 105 us -> 34.6 us
  blocking collectives: 35.3 us -> 69.5 us
    psum x1 -> x0, waiting for transfers between devices: 71.2 us -> none  [per_device(): weight_stack = lax.psum(owner[:, None, None] * own_weights[None], 'rng')]
    all_gather x0 -> x1, blocking collectives: none -> 34.2 us  [per_device(): piece_now = all_gather(block_here, 'rng')]
    unnamed x22 -> x17, local copies, waits for them, and re-layouts: 13.5 us -> 12.1 us
  transfers between devices with their start and end apart: 5 -> 4, of which waited for: 5 -> 4; matrix products, arithmetic and copies ran while one was open for 2% -> 3% of each run, Pallas kernels for 0% -> 0%
where the time goes in v1:
time: 261 us; the launch traced here: 260 us
  other arithmetic  95.7 us (37%)
  blocking collectives  69.5 us (27%)
  waiting for transfers between devices  34.6 us (13%)
  local copies, waits for them, and re-layouts  26.8 us (10%)
  between operations  16.8 us (6%)
  matrix products  16.4 us (6%)
    another operation x10, other arithmetic, solve_weights(): factor = jnp.linalg.cholesky(loaded)  56.4 us
    reduce_scatter x4, waiting for transfers between devices, per_device(): lax.psum_scatter(partial_out, 'chan', scatter_dimension=1, tiled=True)  34.5 us
    all_gather x1, blocking collectives, per_device(): piece_now = all_gather(block_here, 'rng')  34.2 us
    all_gather x1, blocking collectives, per_device(): training = lax.all_gather(training, 'rng', axis=2, tiled=True)  33.1 us
    another operation x3, other arithmetic, solve_weights(): lax.linalg.triangular_solve(factor, forward, left_side=True, lower=True,...  30.4 us
    unnamed x17, local copies, waits for them, and re-layouts  12.1 us
    another operation x15, local copies, waits for them, and re-layouts  8.93 us
    dot_general x8, matrix products, apply_taps(): lax.dot_general(beam_taps, samples, (((0,), (1,)), ((), ())), preferred_e...  7.72 us
  transfers between devices with their start and end apart: 4, of which 4 were waited for; matrix products, arithmetic and copies ran while one was open for 3% of the time, Pallas kernels for 0%

profile of v1, /device:TPU:0, one launch (start us, length us, event | category | flops | bytes accessed | tf_op | source)
XLA Modules:
  0.0 260.1 jit_solution(4678703121463867750)
XLA Ops:
  7.2 0.7 bitcast_or_fusion
  7.9 0.7 compare_and_fusion
  8.6 11.0 %copy.52 = bf16[4,2,2048,96]{3,1,2,0:T(2,128)(2,1)} copy(bf16[4,2,2048,96]{2,3,1,0:T(8,128)(2,1)} %param.4) | data formatting | bytes 6291456 | tf_op args[0]
  19.7 2.9 %gather_fusion = bf16[64,2,96]{2,1,0:T(2,128)(2,1)S(1)} fusion(bf16[4,2,2048,96]{3,1,2,0:T(2,128)(2,1)} %copy.52, s32[64]{0:T(128)S(1)} %reshape.177), kind=kCustom, calls=%fused_computation | custom fusion | bytes 49664 | tf_op jit(solution)/shard_map/vmap(jit(_take))/gather | solution.py:70
  22.9 2.2 all_gather.10
  25.4 33.1 %all_gather.11 = bf16[4,2,128,192]{3,0,1,2:T(4,128)(2,1)S(1)} all-gather(bf16[4,2,16,192]{3,0,1,2:T(4,128)(2,1)S(1)} %copy.55), channel_id=1, replica_groups=mesh['parts'=2,'rng'=8,'chan'=2] {'rng'}, dimensions={2}, use_global_device_ids=true | all-gather | bytes 442368 | tf_op jit(solution)/shard_map/all_gather | solution.py:73
  58.5 0.8 fusion.132
  63.0 0.7 fusion.8
  64.7 11.7 %cholesky.76 = f32[128,128]{1,0:T(8,128)S(1)} custom-call(f32[128,128]{1,0:T(8,128)S(1)} %cholesky.189), custom_call_target="Cholesky" | custom-call | tf_op jit(solution)/shard_map/jit(cholesky)/cholesky | solution.py:47
  76.5 9.8 %custom-call.24 = f32[1,128,128]{1,2,0:T(8,128)S(1)} custom-call(f32[1,128,128]{2,1,0:T(8,128)S(1)} %get-tuple-element.51), custom_call_target="InvertDiagBlocksLowerTriangular" | custom-call | tf_op jit(solution)/shard_map/jit(cholesky)/cholesky | solution.py:47
  86.9 11.9 %cholesky.160 = f32[128,128]{1,0:T(8,128)S(1)} custom-call(f32[128,128]{1,0:T(8,128)S(1)} %cholesky.193), custom_call_target="Cholesky" | custom-call | tf_op jit(solution)/shard_map/jit(cholesky)/cholesky | solution.py:47
  99.1 9.8 %custom-call.25 = f32[1,128,128]{1,2,0:T(8,128)S(1)} custom-call(f32[1,128,128]{2,1,0:T(8,128)S(1)} %get-tuple-element.49), custom_call_target="InvertDiagBlocksLowerTriangular" | custom-call | tf_op jit(solution)/shard_map/jit(cholesky)/cholesky | solution.py:47
  109.3 0.4 convolution_subtract_fusion.1
  109.7 11.7 %cholesky.179 = f32[128,128]{1,0:T(8,128)S(1)} custom-call(f32[128,128]{1,0:T(8,128)S(1)} %convolution_subtract_fusion.1), custom_call_target="Cholesky" | custom-call | tf_op jit(solution)/shard_map/jit(cholesky)/cholesky | solution.py:47
  121.5 0.7 compare_reduce_fusion
  122.3 0.6 compare_reduce_fusion.1
  124.8 0.9 select_select_fusion
  125.7 9.0 %while.1 = (s32[]{:T(128)}, f32[384,384]{0,1:T(8,128)}, s32[3,2]{0,1:T(2,128)S(1)}, f32[3,128,128]{2,1,0:T(8,128)S(1)}, s32[]{:T(128)}) while((s32[]{:T(128)}, f32[384,384]{0,1:T(8,128)}, s32[3,2]{0,1:T(2,128)S(1)}, f32[3,128,128]{2,1,0:T(8,128)S(1)}, s32[]{:T(128)}) %tuple.43), condition=%wide.while_cond, body=%wide.while_body.sunk | while | flops 2 | bytes 393321 | solution.py:49
  125.7 0.5 fusion.143
  126.3 2.5 dynamic-slice.15
  129.0 0.5 fusion.143
  129.5 2.2 dynamic-slice.15
  131.9 0.5 fusion.143
  132.4 2.1 dynamic-slice.15
  134.7 29.5 %custom-call.26 = f32[3,128,128]{1,2,0:T(8,128)S(1)} custom-call(f32[3,128,128]{2,1,0:T(8,128)S(1)} %get-tuple-element.9), custom_call_target="InvertDiagBlocksLowerTriangular" | custom-call | tf_op jit(solution)/shard_map/triangular_solve | solution.py:49
  164.2 0.3 fusion.69
  164.8 1.0 convolution_subtract_fusion.5
  166.0 1.1 convolution_subtract_fusion.4
  167.4 1.1 convolution_subtract_fusion.3
  168.7 1.1 convolution_subtract_fusion.2
  170.4 34.2 %all_gather.12 = f32[8,4,16,384]{3,2,1,0:T(8,128)} all-gather(f32[1,4,16,384]{3,2,1,0:T(8,128)S(1)} %broadcast_multiply_fusion), channel_id=1, replica_groups=mesh['parts'=2,'rng'=8,'chan'=2] {'rng'}, dimensions={0}, use_global_device_ids=true | all-gather | bytes 884736 | tf_op jit(solution)/shard_map/all_gather | solution.py:93
  204.6 1.2 reduce_sum.30
  206.0 0.6 fusion.133
  206.7 1.0 fusion.19
  207.6 1.7 convolution_add_fusion.3
  209.4 1.0 fusion.16
  210.3 1.7 convolution_add_fusion.2
  212.3 1.0 convolution_add_fusion.1
  213.6 1.0 convolution_add_fusion
  214.6 3.5 %reduce-scatter.5.cloned.1.call-done = f32[32,1024]{1,0:T(8,128)} async-done(((f32[32,2048]{1,0:T(8,128)}), f32[32,1024]{1,0:T(8,128)}) %reduce-scatter.5.cloned.1.call-update) | async-done | bytes 131088 | tf_op jit(solution)/shard_map/reduce_scatter | solution.py:106
  218.1 0.9 convert_element_type.85
  219.0 10.2 %reduce-scatter.7.cloned.1.call-done = f32[32,1024]{1,0:T(8,128)} async-done(((f32[32,2048]{1,0:T(8,128)}), f32[32,1024]{1,0:T(8,128)}) %reduce-scatter.7.cloned.1.call-update) | async-done | bytes 131088 | tf_op jit(solution)/shard_map/reduce_scatter | solution.py:106
  229.2 0.9 convert_element_type.87
  230.1 10.2 %reduce-scatter.9.cloned.1.call-done = f32[32,1024]{1,0:T(8,128)} async-done(((f32[32,2048]{1,0:T(8,128)}), f32[32,1024]{1,0:T(8,128)}) %reduce-scatter.9.cloned.1.call-update) | async-done | bytes 131088 | tf_op jit(solution)/shard_map/reduce_scatter | solution.py:106
  240.4 0.9 convert_element_type.89
  241.3 10.6 %reduce-scatter.11.cloned.1.call-done = f32[32,1024]{1,0:T(8,128)} async-done(((f32[32,2048]{1,0:T(8,128)}), f32[32,1024]{1,0:T(8,128)}) %reduce-scatter.11.cloned.1.call-update) | async-done | bytes 131088 | tf_op jit(solution)/shard_map/reduce_scatter | solution.py:106
  251.9 0.9 convert_element_type.91
  252.8 0.7 pad_maximum_fusion
  (94 shorter events, 9.0 us)
Async XLA Ops:
  7.2 211.0 %reduce-scatter.5.cloned.1.call-start = ((), (), s32[]{:S(2)}) async-start(), calls=%async_computation.4 | async-start | bytes 393216 | tf_op jit(solution)/shard_map/reduce_scatter | solution.py:106
  8.6 14.0 %copy-start.3 = (s32[4,16]{1,0:T(4,128)S(1)}, s32[4,16]{1,0:T(4,128)}, u32[]{:S(2)}) copy-start(s32[4,16]{1,0:T(4,128)} %param.6) | copy-start | bytes 772
  86.6 77.6 %copy-start.2 = (s32[4,16]{1,0:T(4,128)S(1)}, s32[4,16]{1,0:T(4,128)}, u32[]{:S(2)}) copy-start(s32[4,16]{1,0:T(4,128)} %param.7) | copy-start | bytes 772
  125.7 81.0 %copy-start = (bf16[4,2,2048,96]{2,3,1,0:T(8,128)(2,1)S(1)}, bf16[4,2,2048,96]{2,3,1,0:T(8,128)(2,1)}, u32[]{:S(2)}) copy-start(bf16[4,2,2048,96]{2,3,1,0:T(8,128)(2,1)} %param.4) | copy-start | bytes 9437188
  205.8 7.5 %copy-start.1 = (f32[4,16,384]{2,1,0:T(8,128)}, f32[4,16,384]{2,1,0:T(8,128)S(1)}, u32[]{:S(2)}) copy-start(f32[4,16,384]{2,1,0:T(8,128)S(1)} %reduce_sum.30) | copy-start | bytes 294916
  209.3 19.9 %reduce-scatter.7.cloned.1.call-start = ((), (), s32[]{:S(2)}) async-start(), calls=%async_computation.5 | async-start | bytes 393216 | tf_op jit(solution)/shard_map/reduce_scatter | solution.py:106
  212.0 28.3 %reduce-scatter.9.cloned.1.call-start = ((), (), s32[]{:S(2)}) async-start(), calls=%async_computation.6 | async-start | bytes 393216 | tf_op jit(solution)/shard_map/reduce_scatter | solution.py:106
  213.3 38.6 %reduce-scatter.11.cloned.1.call-start = ((), (), s32[]{:S(2)}) async-start(), calls=%async_computation.7 | async-start | bytes 393216 | tf_op jit(solution)/shard_map/reduce_scatter | solution.py:106
Sparse Core Ops, SparseCore 0:
  209.4 8.6 reduce-scatter.4
  220.3 8.8 reduce-scatter.6
  231.5 8.8 reduce-scatter.8
  243.0 8.8 reduce-scatter.10
